TPU v7x, 32 devices: a whole 2x2x4 slice. The times are simulated.
32 devices in a mesh: seqa: 4 (over z), seqb: 2 (over x), dp: 4 (over y, core).
Axes of the slice: x: 2, y: 2, z: 4, core: 2. Of those that a mesh axis runs over, the one named last changes fastest.
Arguments:
- queries: bfloat16 [1024, 8, 64], P(('dp', 'seqa', 'seqb')), parts along dimension 0, may hold values from -6 to 6
- keys: bfloat16 [1024, 8, 64], P(('dp', 'seqa', 'seqb')), parts along dimension 0, may hold values from -6 to 6
- values: bfloat16 [1024, 8, 64], P(('dp', 'seqa', 'seqb')), parts along dimension 0, may hold values from -6 to 6
- doc_bounds: int32 [36], P('dp'), parts along dimension 0, may hold values from 0 to 256, as said below
- q_gain: float32 [64], replicated, may hold values from 0.25 to 1.75
- k_gain: float32 [64], replicated, may hold values from 0.25 to 1.75
Outputs:
- attended: bfloat16 [1024, 8, 64], P(('dp', 'seqa', 'seqb')), parts along dimension 0
There are 4 independent parts, one for each index of `dp`. A program takes and returns all parts, laid end to end along the dimension named above; an argument that names none is the same for every part. Nothing has to cross between parts.
Inputs may be any that keep to these rules, and one draw needn't show every extreme that they name: doc_bounds[0] is 0, doc_bounds[8] is 256, and the entries rise strictly.
All inputs are finite; a program needn't handle non-finite values.
Results may differ from a plain program's by a relative error of at most 0.0015.
Values may be sent and summed in bfloat16 or wider, within the bound.
A program may use at most 64 MiB of HBM per device.

v0:
```python
import jax
import jax.numpy as jnp
from jax import lax
from jax.sharding import PartitionSpec as P

TOK_DEV = 32
DOCS = 8


def for_sending(value):
    return jax.tree.map(lambda a: a.astype(jnp.bfloat16) if a.dtype == jnp.float32 else a, value)


def prepare(block, gain, positions):
    values32 = block.astype(jnp.float32)
    scale = lax.rsqrt(jnp.mean(values32 * values32, axis=-1, keepdims=True) + 1e-06)
    normed = values32 * scale * gain
    half = normed.shape[-1] // 2
    freq = jnp.exp(-jnp.log(10000.0) * jnp.arange(half, dtype=jnp.float32) * 2.0 / normed.shape[-1])
    angle = positions.astype(jnp.float32)[:, None] * freq[None, :]
    first = normed[:, :half]
    second = normed[:, half:]
    cosine = jnp.cos(angle)
    sine = jnp.sin(angle)
    rotated = jnp.concatenate(
        [first * cosine - second * sine, first * sine + second * cosine], axis=-1
    )
    return rotated.astype(jnp.bfloat16)


def attend_head(query_head, key_head, value_head, doc_bounds, q_gain, k_gain):
    length, width = query_head.shape
    places = jnp.arange(length, dtype=jnp.int32)
    doc = jnp.sum((places[:, None] >= doc_bounds[None, 1:DOCS]).astype(jnp.int32), axis=1).astype(
        jnp.int32
    )
    positions = places - doc_bounds[doc]
    qr = prepare(query_head, q_gain, positions)
    kr = prepare(key_head, k_gain, positions)
    block = 8 * TOK_DEV
    count = length // block

    def one_block(items):
        query_rows, query_doc, query_place = items
        scores = jnp.dot(query_rows, kr.T, preferred_element_type=jnp.float32) / jnp.sqrt(
            jnp.float32(width)
        )
        allowed = (query_doc[:, None] == doc[None, :]) & (places[None, :] <= query_place[:, None])
        scores = jnp.where(allowed, scores, jnp.float32(-1e30))
        top = jnp.max(scores, axis=1, keepdims=True)
        expo = jnp.where(allowed, jnp.exp(scores - top), jnp.float32(0.0))
        weights = (expo / jnp.sum(expo, axis=1, keepdims=True)).astype(jnp.bfloat16)
        return jnp.dot(weights, value_head, preferred_element_type=jnp.float32).astype(jnp.bfloat16)

    outputs = lax.map(
        one_block,
        (qr.reshape(count, block, width), doc.reshape(count, block), places.reshape(count, block)),
    )
    return outputs.reshape(length, width)


def body(queries, keys, values, doc_bounds, q_gain, k_gain):
    query_full, key_full, value_full = (
        lax.all_to_all(queries, ("seqa", "seqb"), split_axis=1, concat_axis=0, tiled=True),
        lax.all_to_all(keys, ("seqa", "seqb"), split_axis=1, concat_axis=0, tiled=True),
        lax.all_to_all(values, ("seqa", "seqb"), split_axis=1, concat_axis=0, tiled=True),
    )
    attend_all = jax.vmap(attend_head, in_axes=(1, 1, 1, None, None, None), out_axes=1)
    result = attend_all(query_full, key_full, value_full, doc_bounds, q_gain, k_gain)
    back = jax.tree.map(
        lambda part, own: part.astype(own.dtype),
        lax.all_to_all(
            for_sending(result), ("seqa", "seqb"), split_axis=0, concat_axis=1, tiled=True
        ),
        result,
    )
    return back


def solution(mesh):
    placed = (
        P(("dp", "seqa", "seqb"), None, None),
        P(("dp", "seqa", "seqb"), None, None),
        P(("dp", "seqa", "seqb"), None, None),
        P("dp"),
        P(),
        P(),
    )
    return jax.shard_map(
        body,
        mesh=mesh,
        in_specs=placed,
        out_specs=P(("dp", "seqa", "seqb"), None, None),
        check_vma=False,
    )
```

profile of v0, /device:TPU:0, one launch (start us, length us, event | category | flops | bytes accessed | tf_op | source)
XLA Modules:
  0.0 51.4 jit_solution(5390356876942272930)
XLA Ops:
  0.0 0.8 %copy.39 = bf16[32,8,64]{2,0,1:T(8,128)(2,1)S(1)} copy(bf16[32,8,64]{2,1,0:T(8,128)(2,1)} %param.6) | data formatting | bytes 65536 | tf_op args[0]
  0.9 0.7 %reshape.437 = bf16[8,2,1024]{2,1,0:T(2,128)(2,1)} reshape(bf16[8,32,64]{2,1,0:T(8,128)(2,1)S(1)} %bitcast.69) | data formatting | bytes 65536
  1.6 7.4 %all-to-all-start = ((bf16[8,2,1024]{2,1,0:T(2,128)(2,1)}), bf16[8,2,1024]{2,1,0:T(2,128)(2,1)S(1)}, u32[]{:S(2)}, u32[]{:S(2)}) async-start(bf16[8,2,1024]{2,1,0:T(2,128)(2,1)} %reshape.437), calls=%async_computation | async-start | bytes 65536 | tf_op jit(solution)/shard_map/all_to_all | solution.py:64
  9.0 0.7 %fusion.35 = (s32[1]{0:T(128)}, s32[1]{0:T(128)}, s32[1]{0:T(128)}, s32[1]{0:T(128)}, s32[1]{0:T(128)}, /*index=5*/s32[1]{0:T(128)}, s32[1]{0:T(128)}, s32[1]{0:T(128)}, s32[1]{0:T(128)}) fusion(s32[9]{0:T(128)S(1)} %copy-done.2), kind=kLoop, calls=%fused_computation.61 | loop fusion | bytes 72 | tf_op jit(solution)/shard_map/vmap()/gather | solution.py:37
  9.8 0.1 convert_reduce_fusion
  9.9 0.7 %reshape.439 = bf16[8,2,1024]{2,1,0:T(2,128)(2,1)} reshape(bf16[8,32,64]{2,1,0:T(8,128)(2,1)S(1)} %bitcast.70) | data formatting | bytes 65536
  10.7 0.1 copy-done.1
  10.8 0.7 %reshape.435 = bf16[8,2,1024]{2,1,0:T(2,128)(2,1)} reshape(bf16[8,32,64]{2,1,0:T(8,128)(2,1)S(1)} %bitcast.71) | data formatting | bytes 65536
  11.5 4.4 %compare_select_fusion.1 = s32[256,1]{0,1:T(1,128)S(1)} fusion(s32[]{:T(128)} %bitcast.7, s32[]{:T(128)} %bitcast.8, s32[]{:T(128)} %bitcast.9, s32[]{:T(128)} %bitcast.10, s32[]{:T(128)} %bitcast.11, s32[]{:T(128)} %bitcast.13, s32[]{:T(128)} %bitcast.12, s32[256,1]{0,1:T(1,128)S(1)} %bitcast.74), kind=kLoop, calls=%fused_computation.50 | loop fusion | flops 3840 | bytes 2076 | tf_op jit(solution)/shard_map/vmap()/gather | solution.py:37
  15.9 1.2 %fusion.32 = f32[256]{0:T(256)S(1)} fusion(pred[256]{0:T(512)(128)(4,1)S(1)} %get-tuple-element.22, pred[256]{0:T(512)(128)(4,1)S(1)} %get-tuple-element.21, s32[256]{0:T(256)S(1)} %bitcast.75, s32[]{:T(128)} %bitcast.5, s32[]{:T(128)} %bitcast.6), kind=kLoop, calls=%fused_computation.57 | loop fusion | flops 1024 | bytes 2568 | tf_op jit(solution)/shard_map/vmap()/convert_element_type | solution.py:20
  17.1 6.0 %all-to-all-start.1 = ((bf16[8,2,1024]{2,1,0:T(2,128)(2,1)}), bf16[8,2,1024]{2,1,0:T(2,128)(2,1)S(1)}, u32[]{:S(2)}, u32[]{:S(2)}) async-start(bf16[8,2,1024]{2,1,0:T(2,128)(2,1)} %reshape.439), calls=%async_computation.1 | async-start | bytes 65536 | tf_op jit(solution)/shard_map/all_to_all | solution.py:65
  23.2 0.1 reshape.438
  23.3 0.1 multiply_reduce_fusion.1
  23.6 6.2 %all-to-all-done.1 = bf16[8,2,1024]{2,1,0:T(2,128)(2,1)S(1)} async-done(((bf16[8,2,1024]{2,1,0:T(2,128)(2,1)}), bf16[8,2,1024]{2,1,0:T(2,128)(2,1)S(1)}, u32[]{:S(2)}, u32[]{:S(2)}) %all-to-all-start.1) | async-done | bytes 32800 | tf_op jit(solution)/shard_map/all_to_all | solution.py:65
  29.8 3.3 %all-to-all-start.2 = ((bf16[8,2,1024]{2,1,0:T(2,128)(2,1)}), bf16[8,2,1024]{2,1,0:T(2,128)(2,1)S(1)}, u32[]{:S(2)}, u32[]{:S(2)}) async-start(bf16[8,2,1024]{2,1,0:T(2,128)(2,1)} %reshape.435), calls=%async_computation.2 | async-start | bytes 65536 | tf_op jit(solution)/shard_map/all_to_all | solution.py:66
  33.2 0.1 reshape.440
  33.3 0.1 multiply_reduce_fusion
  33.7 0.6 %copy-done.3 = f32[64]{0:T(128)S(1)} copy-done((f32[64]{0:T(128)S(1)}, f32[64]{0:T(128)}, u32[]{:S(2)}) %copy-start.3) | copy-done | bytes 280
  34.3 0.1 fusion.20
  34.4 0.6 %fusion.29 = (bf16[256,32]{1,0:T(8,128)(2,1)S(1)}, bf16[256,32]{1,0:T(8,128)(2,1)S(1)}, bf16[256,32]{1,0:T(8,128)(2,1)S(1)}, bf16[256,32]{1,0:T(8,128)(2,1)S(1)}) fusion(f32[1,256,64]{2,1,0:T(8,128)S(1)} %get-tuple-element.51, f32[32]{0:T(128)S(1)} %multiply_exponential_fusion, f32[256]{0:T(256)S(1)} %fusion.32, f32[1,256,64]{2,1,0:T(8,128)S(1)} %get-tuple-element.52), kind=kLoop, calls=%fused_computation.40 | loop fusion | flops 139264 | bytes 197760 | tf_op jit(solution)/shard_map/vmap()/concatenate | solution.py:25
  35.0 0.3 fusion.36
  35.3 0.1 fusion.11
  35.4 4.4 %all-to-all-done.2 = bf16[8,2,1024]{2,1,0:T(2,128)(2,1)S(1)} async-done(((bf16[8,2,1024]{2,1,0:T(2,128)(2,1)}), bf16[8,2,1024]{2,1,0:T(2,128)(2,1)S(1)}, u32[]{:S(2)}, u32[]{:S(2)}) %all-to-all-start.2) | async-done | bytes 32800 | tf_op jit(solution)/shard_map/all_to_all | solution.py:66
  39.8 0.1 reshape.436
  39.9 0.2 fusion.1
  40.2 0.5 broadcast.313
  40.7 0.7 %reduce.16 = bf16[256,64]{0,1:T(8,128)(2,1)S(1)} reduce(bf16[256,1,64]{0,2,1:T(8,128)(2,1)S(1)} %fusion.1, bf16[]{:T(256)} %broadcast.313), dimensions={1}, to_apply=%copy.29.reduce_sub_computation | reduce | bytes 65538 | tf_op jit(solution)/shard_map/vmap()/transpose;vmap()/reshape;vmap()/transpose | solution.py:69
  41.4 0.1 copy.40
  41.5 0.1 reshape.441
  41.6 9.1 %all_to_all.51 = bf16[8,2,1024]{2,1,0:T(2,128)(2,1)S(1)} all-to-all(bf16[8,2,1024]{2,1,0:T(2,128)(2,1)S(1)} %reshape.441), channel_id=1, replica_groups=mesh['seqa'=4,'seqb'=2,'dp'=4] {'seqa','seqb'}, dimensions={0} | all-to-all | bytes 65536 | tf_op jit(solution)/shard_map/all_to_all | solution.py:72
  50.7 0.1 reshape.442
  50.8 0.7 %copy.30 = bf16[32,8,64]{2,1,0:T(8,128)(2,1)} copy(bf16[32,8,64]{2,0,1:T(8,128)(2,1)S(1)} %bitcast.68) | data formatting | bytes 65536 | tf_op jit(solution)/shard_map/all_to_all | solution.py:72
  (23 shorter events, 0.6 us)
Async XLA Ops:
  0.9 8.2 %copy-start.2 = (s32[9]{0:T(128)S(1)}, s32[9]{0:T(128)}, u32[]{:S(2)}) copy-start(s32[9]{0:T(128)} %param.9) | copy-start | bytes 112
  1.6 8.3 %copy-start = (bf16[32,8,64]{2,1,0:T(8,128)(2,1)S(1)}, bf16[32,8,64]{2,1,0:T(8,128)(2,1)}, u32[]{:S(2)}) copy-start(bf16[32,8,64]{2,1,0:T(8,128)(2,1)} %param.7) | copy-start | bytes 98308
  1.6 15.6 %all-to-all-start = ((bf16[8,2,1024]{2,1,0:T(2,128)(2,1)}), bf16[8,2,1024]{2,1,0:T(2,128)(2,1)S(1)}, u32[]{:S(2)}, u32[]{:S(2)}) async-start(bf16[8,2,1024]{2,1,0:T(2,128)(2,1)} %reshape.437), calls=%async_computation | async-start | bytes 65536 | tf_op jit(solution)/shard_map/all_to_all | solution.py:64
  9.9 0.8 %copy-start.1 = (bf16[32,8,64]{2,1,0:T(8,128)(2,1)S(1)}, bf16[32,8,64]{2,1,0:T(8,128)(2,1)}, u32[]{:S(2)}) copy-start(bf16[32,8,64]{2,1,0:T(8,128)(2,1)} %param.8) | copy-start | bytes 98308
  17.1 12.7 %all-to-all-start.1 = ((bf16[8,2,1024]{2,1,0:T(2,128)(2,1)}), bf16[8,2,1024]{2,1,0:T(2,128)(2,1)S(1)}, u32[]{:S(2)}, u32[]{:S(2)}) async-start(bf16[8,2,1024]{2,1,0:T(2,128)(2,1)} %reshape.439), calls=%async_computation.1 | async-start | bytes 65536 | tf_op jit(solution)/shard_map/all_to_all | solution.py:65
  29.8 10.0 %all-to-all-start.2 = ((bf16[8,2,1024]{2,1,0:T(2,128)(2,1)}), bf16[8,2,1024]{2,1,0:T(2,128)(2,1)S(1)}, u32[]{:S(2)}, u32[]{:S(2)}) async-start(bf16[8,2,1024]{2,1,0:T(2,128)(2,1)} %reshape.435), calls=%async_computation.2 | async-start | bytes 65536 | tf_op jit(solution)/shard_map/all_to_all | solution.py:66
  33.6 0.7 %copy-start.3 = (f32[64]{0:T(128)S(1)}, f32[64]{0:T(128)}, u32[]{:S(2)}) copy-start(f32[64]{0:T(128)} %param.11) | copy-start | bytes 772
  33.6 0.7 %copy-start.4 = (f32[64]{0:T(128)S(1)}, f32[64]{0:T(128)}, u32[]{:S(2)}) copy-start(f32[64]{0:T(128)} %param.10) | copy-start | bytes 772
where the time goes:
time: 52 us; the launch traced here: 51.4 us
  starting transfers between devices  16.8 us (32%)
  waiting for transfers between devices  10.6 us (20%)
  blocking collectives  9.06 us (17%)
  other arithmetic  7.48 us (14%)
  local copies, waits for them, and re-layouts  6.8 us (13%)
  matrix products  0.54 us (1%)
    all_to_all x1, blocking collectives, body(): lax.all_to_all(for_sending(result), ('seqa', 'seqb'), split_axis=0, conca...  9.06 us
    all_to_all x1, starting transfers between devices, body(): lax.all_to_all(queries, ('seqa', 'seqb'), split_axis=1, concat_axis=0, ti...  7.45 us
    all_to_all x1, waiting for transfers between devices, body(): lax.all_to_all(keys, ('seqa', 'seqb'), split_axis=1, concat_axis=0, tiled...  6.22 us
    all_to_all x1, starting transfers between devices, body(): lax.all_to_all(keys, ('seqa', 'seqb'), split_axis=1, concat_axis=0, tiled...  6 us
    unnamed x25, local copies, waits for them, and re-layouts  4.6 us
    gather x2, other arithmetic, attend_head(): positions = places - doc_bounds[doc]  4.39 us
    all_to_all x1, waiting for transfers between devices, body(): lax.all_to_all(values, ('seqa', 'seqb'), split_axis=1, concat_axis=0, til...  4.37 us
    all_to_all x1, starting transfers between devices, body(): lax.all_to_all(values, ('seqa', 'seqb'), split_axis=1, concat_axis=0, til...  3.34 us
  transfers between devices with their start and end apart: 3, of which 2 were waited for; matrix products, arithmetic and copies ran while one was open for 19% of the time, Pallas kernels for 0%

commit v1 on v0

--- a/solution.py
+++ b/solution.py
@@ -1,10 +1,190 @@
+import functools
+
 import jax
 import jax.numpy as jnp
 from jax import lax
+from jax.experimental import pallas as pl
+from jax.experimental.pallas import tpu as pltpu
 from jax.sharding import PartitionSpec as P
 
+MESH = pl.DeviceIdType.MESH
 TOK_DEV = 32
 DOCS = 8
+
+
+def cos_sin(angle):
+    turns = jnp.floor(angle * 0.6366197723675814 + 0.5)
+    r = angle - turns * 1.5703125
+    r = r - turns * 4.837512969970703125e-4
+    r = r - turns * 7.54978995489188216e-8
+    z = r * r
+    s = ((-1.9515295891e-4 * z + 8.3321608736e-3) * z - 1.6666654611e-1) * z * r + r
+    c = ((2.443315711809948e-5 * z - 1.388731625493765e-3) * z + 4.166664568298827e-2) * z * z
+    c = c - 0.5 * z + 1.0
+    quarter = turns.astype(jnp.int32)
+    odd = (quarter & 1) == 1
+    cosine = jnp.where(odd, s, c)
+    sine = jnp.where(odd, c, s)
+    cosine = jnp.where(((quarter + 1) & 2) == 2, -cosine, cosine)
+    sine = jnp.where((quarter & 2) == 2, -sine, sine)
+    return cosine, sine
+
+
+def starts_of(places, doc):
+    start = jnp.zeros_like(places)
+    for d in range(1, doc.shape[0] - 1):
+        start = jnp.where(places >= doc[d], doc[d], start)
+    return start
+
+
+def kernel(
+    nb, q_hbm, k_hbm, v_hbm, doc_hbm, qg_hbm, kg_hbm, out_ref,
+    qb, kb, vb, doc, qg, kg, rows_qk, rows_v, send, recv, back, gathered, rows_out,
+    in_sem, send_sem, recv_sem, back_send, back_recv,
+):
+    tok, heads, width = qb.shape
+    n = recv.shape[0]
+    half, pair = tok // 2, 2 * width
+    me = lax.axis_index("seqa") * nb + lax.axis_index("seqb")
+
+    def place(m):
+        peer = lax.rem(me + m, n)
+        return peer, {"seqa": peer // nb, "seqb": lax.rem(peer, nb)}
+
+    barrier = pltpu.get_barrier_semaphore()
+    for m in range(1, n):
+        pl.semaphore_signal(barrier, inc=1, device_id=place(m)[1], device_id_type=MESH)
+    loads = [
+        pltpu.make_async_copy(src, dst, in_sem.at[i])
+        for i, (src, dst) in enumerate(
+            ((doc_hbm, doc), (qg_hbm, qg), (kg_hbm, kg), (q_hbm, qb), (k_hbm, kb), (v_hbm, vb))
+        )
+    ]
+    for load in loads:
+        load.start()
+    for load in loads[:3]:
+        load.wait()
+
+    lane = lax.broadcasted_iota(jnp.int32, (tok, pair), 1)
+    low = lane < width
+    places = me * tok + lax.broadcasted_iota(jnp.int32, (tok, pair), 0)
+    within = lax.rem(lane, width // 2).astype(jnp.float32)
+    freq = jnp.exp(within * (-2.0 / width * 9.210340371976184))
+    cosine, sine = cos_sin((places - starts_of(places, doc)).astype(jnp.float32) * freq)
+    first = lax.rem(lane, width) < width // 2
+    sine = jnp.where(first, -sine, sine)
+    gain = jnp.concatenate([qg[...] * width**-0.5, kg[...]], axis=-1)
+
+    for load in loads[3:]:
+        load.wait()
+    rows_qk[:, :width] = qb[...].astype(jnp.float32).reshape(tok * heads, width)
+    rows_qk[:, width:] = kb[...].astype(jnp.float32).reshape(tok * heads, width)
+    rows_v[...] = vb[...].astype(jnp.float32).reshape(tok * heads, width)
+    for h in range(heads):
+        x = rows_qk[pl.ds(h, tok, stride=heads), :]
+        v = rows_v[pl.ds(h, tok, stride=heads), :]
+        square = x * x
+        total_q = jnp.sum(jnp.where(low, square, 0.0), axis=-1, keepdims=True)
+        total_k = jnp.sum(jnp.where(low, 0.0, square), axis=-1, keepdims=True)
+        x = x * lax.rsqrt(jnp.where(low, total_q, total_k) / width + 1e-06) * gain
+        other = jnp.where(
+            first, pltpu.roll(x, pair - width // 2, 1), pltpu.roll(x, width // 2, 1)
+        )
+        x = x * cosine + other * sine
+        kv = jnp.concatenate([x[:, width:], v], axis=-1)
+        qq = jnp.concatenate([x[:half, :width], x[half:, :width]], axis=-1)
+        send[h, :tok, :] = kv.astype(jnp.bfloat16)
+        send[h, tok:, :] = qq.astype(jnp.bfloat16)
+    recv[me] = send[me]
+
+    q_places = [
+        lax.broadcasted_iota(jnp.int32, (n, half, 1), 0) * tok
+        + lax.broadcasted_iota(jnp.int32, (n, half, 1), 1)
+        + part * half
+        for part in range(2)
+    ]
+    q_places = [x.reshape(n * half, 1) for x in q_places]
+    q_starts = [starts_of(x, doc) for x in q_places]
+
+    pl.semaphore_wait(barrier, n - 1)
+
+    def exchange(source, target, sems, m):
+        peer, coords = place(m)
+        return pltpu.make_async_remote_copy(
+            src_ref=source.at[peer],
+            dst_ref=target.at[me],
+            send_sem=sems[0].at[m - 1],
+            recv_sem=sems[1].at[m - 1],
+            device_id=coords,
+            device_id_type=MESH,
+        )
+
+    out = [exchange(send, recv, (send_sem, recv_sem), m) for m in range(1, n)]
+    for copy in out:
+        copy.start()
+    for copy in out:
+        copy.wait_recv()
+
+    outs = []
+    for part in range(2):
+        kv = recv[:, :tok, :].reshape(n * tok, pair)
+        q = recv[:, tok:, part * width : (part + 1) * width].reshape(n * half, width)
+        scores = lax.dot_general(
+            q, kv[:, :width], (((1,), (1,)), ((), ())), preferred_element_type=jnp.float32
+        )
+        key = lax.broadcasted_iota(jnp.int32, scores.shape, 1)
+        allowed = (key >= q_starts[part]) & (key <= q_places[part])
+        expo = jnp.where(allowed, jnp.exp(scores), 0.0)
+        weights = (expo * (1.0 / jnp.sum(expo, axis=1, keepdims=True))).astype(jnp.bfloat16)
+        both = jnp.dot(weights, kv, preferred_element_type=jnp.float32)
+        outs.append(both[:, width:])
+    back[...] = (
+        jnp.concatenate(outs, axis=-1).astype(jnp.bfloat16).reshape(n, half, pair)
+    )
+    home = [exchange(back, gathered, (back_send, back_recv), m) for m in range(1, n)]
+    for copy in home:
+        copy.start()
+    gathered[me] = back[me]
+    for copy in out:
+        copy.wait_send()
+    for copy in home:
+        copy.wait_recv()
+    for h in range(heads):
+        block = gathered[h].astype(jnp.float32)
+        rows_out[pl.ds(h, half, stride=heads), :] = block[:, :width]
+        rows_out[pl.ds(half * heads + h, half, stride=heads), :] = block[:, width:]
+    out_ref[...] = rows_out[...].reshape(tok, heads, width).astype(jnp.bfloat16)
+    for copy in home:
+        copy.wait_send()
+
+
+def fused(n, nb, queries, keys, values, doc_bounds, q_gain, k_gain):
+    tok, heads, width = queries.shape
+    half, pair = tok // 2, 2 * width
+    block = pltpu.VMEM((tok, heads, width), jnp.bfloat16)
+    dma = pltpu.SemaphoreType.DMA((n - 1,))
+    return pl.pallas_call(
+        functools.partial(kernel, nb),
+        out_shape=jax.ShapeDtypeStruct(queries.shape, queries.dtype),
+        in_specs=[pl.BlockSpec(memory_space=pl.ANY)] * 6,
+        out_specs=pl.BlockSpec(memory_space=pltpu.VMEM),
+        scratch_shapes=[
+            block, block, block,
+            pltpu.SMEM(doc_bounds.shape, jnp.int32),
+            pltpu.VMEM((1, width), jnp.float32),
+            pltpu.VMEM((1, width), jnp.float32),
+            pltpu.VMEM((tok * heads, pair), jnp.float32),
+            pltpu.VMEM((tok * heads, width), jnp.float32),
+            pltpu.VMEM((n, tok + half, pair), jnp.bfloat16),
+            pltpu.VMEM((n, tok + half, pair), jnp.bfloat16),
+            pltpu.VMEM((n, half, pair), jnp.bfloat16),
+            pltpu.VMEM((n, half, pair), jnp.bfloat16),
+            pltpu.VMEM((tok * heads, width), jnp.float32),
+            pltpu.SemaphoreType.DMA((6,)),
+            dma, dma, dma, dma,
+        ],
+        compiler_params=pltpu.CompilerParams(collective_id=0, has_side_effects=True),
+    )(queries, keys, values, doc_bounds, q_gain.reshape(1, width), k_gain.reshape(1, width))
 
 
 def for_sending(value):
@@ -86,8 +266,17 @@
         P(),
         P(),
     )
+    nb = mesh.shape["seqb"]
+    n = mesh.shape["seqa"] * nb
+
+    def local(queries, keys, values, doc_bounds, q_gain, k_gain):
+        tok, heads, width = queries.shape
+        fits = heads == n and heads == 8 and tok % 32 == 0 and n * tok <= 512 and width == 64
+        step = functools.partial(fused, n, nb) if fits else body
+        return step(queries, keys, values, doc_bounds, q_gain, k_gain)
+
     return jax.shard_map(
-        body,
+        local,
         mesh=mesh,
         in_specs=placed,
         out_specs=P(("dp", "seqa", "seqb"), None, None),

time: 52 us -> 18 us (0.35)
  starting transfers between devices: 16.8 us -> 0 us
  Pallas kernels: 0 us -> 16.3 us
  waiting for transfers between devices: 10.6 us -> 0 us
  blocking collectives: 9.06 us -> 0 us
  other arithmetic: 7.48 us -> 0 us
  local copies, waits for them, and re-layouts: 6.8 us -> 1.47 us
  matrix products: 0.54 us -> 0 us
    all_to_all x3 -> x0, starting transfers between devices: 16.8 us -> none  [the longest x1 7.45 us: body(): lax.all_to_all(queries, ('seqa', 'seqb'), split_axis=1, concat_axis=0, ti...]
    pallas_call x0 -> x1, Pallas kernels: none -> 16.3 us  [fused(): pl.pallas_call(functools.partial(kernel, nb), out_shape=jax.ShapeDtypeStr...]
    all_to_all x3 -> x0, waiting for transfers between devices: 10.6 us -> none  [the longest x1 6.22 us: body(): lax.all_to_all(keys, ('seqa', 'seqb'), split_axis=1, concat_axis=0, tiled...]
    all_to_all x1 -> x0, blocking collectives: 9.06 us -> none  [body(): lax.all_to_all(for_sending(result), ('seqa', 'seqb'), split_axis=0, conca...]
    gather x2 -> x0, other arithmetic: 4.39 us -> none  [attend_head(): positions = places - doc_bounds[doc]]
    unnamed x25 -> x1, local copies, waits for them, and re-layouts: 4.6 us -> 1.47 us
    convert_element_type x1 -> x0, other arithmetic: 1.23 us -> none  [prepare(): angle = positions.astype(jnp.float32)[:, None] * freq[None, :]]
    gather x1 -> x0, local copies, waits for them, and re-layouts: 0.68 us -> none  [attend_head(): positions = places - doc_bounds[doc]]
  transfers between devices with their start and end apart: 3 -> 0, of which waited for: 2 -> 0; matrix products, arithmetic and copies ran while one was open for 19% -> 0% of each run, Pallas kernels for 0% -> 0%
where the time goes in v1:
time: 18 us; the launch traced here: 17.8 us
  Pallas kernels  16.3 us (91%)
  local copies, waits for them, and re-layouts  1.47 us (8%)
    pallas_call x1, Pallas kernels, fused(): pl.pallas_call(functools.partial(kernel, nb), out_shape=jax.ShapeDtypeStr...  16.3 us
    unnamed x1, local copies, waits for them, and re-layouts  1.47 us

profile of v1, /device:TPU:0, one launch (start us, length us, event | category | flops | bytes accessed | tf_op | source)
XLA Modules:
  0.0 17.8 jit_solution(10423272887484509854)
XLA Ops:
  0.0 16.3 %shard_map.64 = bf16[32,8,64]{2,1,0:T(8,128)(2,1)} custom-call(bf16[32,8,64]{2,1,0:T(8,128)(2,1)} %q_hbm.1, bf16[32,8,64]{2,1,0:T(8,128)(2,1)} %k_hbm.1, bf16[32,8,64]{2,1,0:T(8,128)(2,1)} %v_hbm.1, s32[9]{0:T(128)} %doc_hbm.1, f32[1,64]{1,0:T(1,128)} %bitcast.2, f32[1,64]{1,0:T(1,128)} %bitcast.3), custom_call_target="tpu_custom_call" | custom-call | tf_op jit(solution)/shard_map/pallas_call | solution.py:166
  16.3 1.5 %copy.8 = bf16[32,8,64]{2,1,0:T(8,128)(2,1)} copy(bf16[32,8,64]{2,1,0:T(8,128)(2,1)} %shard_map.64) | data formatting | bytes 65536
